TPU v7x, 32 devices: a whole 2x2x4 slice. The times are simulated.
32 devices in a mesh: row: 4 (over x, core), col: 8 (over z, y).
Axes of the slice: x: 2, y: 2, z: 4, core: 2. Of those that a mesh axis runs over, the one named last changes fastest.
Arguments:
- x_rows: float32 [16, 16384], P(None, ('row', 'col')), may hold values from -6 to 6
- alpha_rows: float32 [16384], P(('row', 'col')), may hold values from -0.5 to 1.5
- x_cols: float32 [16, 8192], P(None, ('col', 'row')), may hold values from -6 to 6
- alpha_cols: float32 [8192], P(('col', 'row')), may hold values from -0.0073242188 to 0.021972656
- lengthscale: float32 [16], replicated, may hold values from 1.2 to 2.5
Outputs:
- row_terms: float32 [16, 16384], P(None, ('row', 'col'))
- kernel_alpha: float32 [16384], P(('row', 'col'))
- grad: float32 [16], replicated
All inputs are finite; a program needn't handle non-finite values.
Results may differ from a plain program's by a relative error of at most 0.00021.
Values sent between devices are 32-bit elements; how exact they have to be, the bound alone decides.
A program may use at most 64 MiB of HBM per device.

v0:
```python
import jax
import jax.numpy as jnp
from jax import lax
from jax.sharding import PartitionSpec as P


def fold_terms(partials, row_scaled, row_alpha):
    dims = row_scaled.shape[0]
    weight_sum = partials[0]
    first_moment = partials[1 : 1 + dims]
    second_moment = partials[1 + dims :]
    terms = (
        0.5
        * row_alpha[None, :]
        * (
            row_scaled * row_scaled * weight_sum[None, :]
            - 2.0 * row_scaled * first_moment
            + second_moment
        )
    )
    return (terms, weight_sum)


def on_device(x_rows, alpha_rows, x_cols, alpha_cols, lengthscale):
    dims = x_rows.shape[0]
    inverse_scale = 1.0 / lengthscale
    own_scaled = x_rows * inverse_scale[:, None]
    own_rows = jnp.concatenate([own_scaled, alpha_rows[None, :]], 0)
    gathered = lax.all_gather(own_rows, "col", axis=1, tiled=True)
    row_scaled = gathered[:dims]
    row_alpha = gathered[dims]
    row_count = row_scaled.shape[1]
    block_rows = min(512, row_count)
    block_count = row_count // block_rows
    row_norms = jnp.sum(row_scaled * row_scaled, 0)
    own_cols = jnp.concatenate([x_cols * inverse_scale[:, None], alpha_cols[None, :]], 0)
    empty = jnp.zeros((2 * dims + 1, row_count), jnp.float32)
    shard_piece = lax.all_gather(own_cols, "row", axis=1, tiled=True)
    col_scaled = shard_piece[:dims]
    col_alpha = shard_piece[dims]
    col_norms = jnp.sum(col_scaled * col_scaled, 0)
    values = jnp.concatenate(
        [
            col_alpha[None, :],
            col_alpha[None, :] * col_scaled,
            col_alpha[None, :] * col_scaled * col_scaled,
        ],
        0,
    )

    def add_block(block_index, carried):
        offset = block_index * block_rows
        row_block = lax.dynamic_slice_in_dim(row_scaled, offset, block_rows, 1)
        block_norms = lax.dynamic_slice_in_dim(row_norms, offset, block_rows, 0)
        cross = lax.dot_general(
            row_block,
            col_scaled,
            (((0,), (0,)), ((), ())),
            precision=lax.Precision.HIGHEST,
            preferred_element_type=jnp.float32,
        )
        kernel = jnp.exp(-0.5 * (block_norms[:, None] + col_norms[None, :] - 2.0 * cross))
        contrib = lax.dot_general(
            values,
            kernel,
            (((1,), (1,)), ((), ())),
            precision=lax.Precision.HIGHEST,
            preferred_element_type=jnp.float32,
        )
        earlier = lax.dynamic_slice_in_dim(carried, offset, block_rows, 1)
        return lax.dynamic_update_slice_in_dim(carried, earlier + contrib, offset, 1)

    partials = lax.fori_loop(0, block_count, add_block, empty)
    summed = lax.psum_scatter(partials, "col", scatter_dimension=1, tiled=True)
    row_terms, kernel_alpha = fold_terms(summed, own_scaled, alpha_rows)
    tile_terms, tile_sum = fold_terms(partials, row_scaled, row_alpha)
    total_rows = row_count * lax.axis_size("row")
    grad = lax.psum(jnp.sum(tile_terms, 1), ("row", "col")) / total_rows
    return (row_terms, kernel_alpha, grad)


def solution(mesh):
    return jax.shard_map(
        on_device,
        mesh=mesh,
        in_specs=(
            P(None, ("row", "col")),
            P(("row", "col")),
            P(None, ("col", "row")),
            P(("col", "row")),
            P(),
        ),
        out_specs=(P(None, ("row", "col")), P(("row", "col")), P()),
        check_vma=False,
    )
```

profile of v0, /device:TPU:0, one launch (start us, length us, event | category | flops | bytes accessed | tf_op | source)
XLA Modules:
  0.0 159.6 jit_solution(6759463865752624172)
XLA Ops:
  9.3 6.3 %all_gather.7 = f32[17,1024]{1,0:T(8,128)S(1)} all-gather(f32[17,256]{1,0:T(8,128)S(1)} %pad_maximum_fusion.2), channel_id=1, replica_groups=mesh['row'=4,'col'=8] {'row'}, dimensions={1}, use_global_device_ids=true | all-gather | bytes 87040 | tf_op jit(solution)/shard_map/all_gather | solution.py:38
  17.2 32.0 %all_gather.6 = f32[17,4096]{1,0:T(8,128)S(1)} all-gather(f32[17,512]{1,0:T(8,128)S(1)} %pad_maximum_fusion.1), channel_id=1, replica_groups=mesh['row'=4,'col'=8] {'col'}, dimensions={1}, use_global_device_ids=true | all-gather | bytes 313344 | tf_op jit(solution)/shard_map/all_gather | solution.py:29
  49.4 35.8 %while.13 = (s32[]{:T(128)}, f32[33,4096]{1,0:T(8,128)S(1)}, f32[4096]{0:T(1024)S(1)}, f32[1024]{0:T(1024)S(1)}, f32[16,4096]{1,0:T(8,128)S(1)}, /*index=5*/f32[...) while((s32[]{:T(128)}, f32[33,4096]{1,0:T(8,128)S(1)}, ...), condition=%wide.region_3.0_spmd, body=%wide.region_2.0_spmd.sunk | while | flops 310395392 | bytes 4630695 | solution.py:73
  49.4 1.8 %fusion.40 = f32[512,1024]{1,0:T(8,128)S(1)} fusion(f32[16,1024]{1,0:T(8,128)S(1)} %get-tuple-element.218, f32[16,4096]{1,0:T(8,128)S(1)} %get-tuple-element.217, s32[]{:T(128)S(6)} %select_n.11), kind=kOutput, calls=%fused_computation.13.clone.1 | convolution fusion | flops 100663296 | bytes 2195460 | tf_op jit(solution)/shard_map/while/body/eval_jaxpr/dot_general | solution.py:55
  51.3 2.5 %fusion.41 = f32[33,4096]{1,0:T(8,128)S(1)} fusion(f32[33,4096]{1,0:T(8,128)S(1)} %get-tuple-element.203, s32[]{:T(128)S(6)} %select_n.11, f32[33,1024]{1,0:T(8,128)S(1)} %get-tuple-element.219, f32[512,1024]{1,0:T(8,128)S(1)} %fusion.40, f32[1024]{0:T(1024)S(1)} %get-tuple-element.216, f32[512]{0:T(512)S(1)} %dynamic_slice.29), kind=kOutput, calls=%fused_computation.8.clone.1 | convolution fusion | flops 209732096 | bytes 2430980 | tf_op jit(solution)/shard_map/while/body/eval_jaxpr/dot_general | solution.py:63
  53.9 1.8 %fusion.40 = f32[512,1024]{1,0:T(8,128)S(1)} fusion(f32[16,1024]{1,0:T(8,128)S(1)} %get-tuple-element.218, f32[16,4096]{1,0:T(8,128)S(1)} %get-tuple-element.217, s32[]{:T(128)S(6)} %select_n.11), kind=kOutput, calls=%fused_computation.13.clone.1 | convolution fusion | flops 100663296 | bytes 2195460 | tf_op jit(solution)/shard_map/while/body/eval_jaxpr/dot_general | solution.py:55
  55.8 2.5 %fusion.41 = f32[33,4096]{1,0:T(8,128)S(1)} fusion(f32[33,4096]{1,0:T(8,128)S(1)} %get-tuple-element.203, s32[]{:T(128)S(6)} %select_n.11, f32[33,1024]{1,0:T(8,128)S(1)} %get-tuple-element.219, f32[512,1024]{1,0:T(8,128)S(1)} %fusion.40, f32[1024]{0:T(1024)S(1)} %get-tuple-element.216, f32[512]{0:T(512)S(1)} %dynamic_slice.29), kind=kOutput, calls=%fused_computation.8.clone.1 | convolution fusion | flops 209732096 | bytes 2430980 | tf_op jit(solution)/shard_map/while/body/eval_jaxpr/dot_general | solution.py:63
  58.3 1.8 %fusion.40 = f32[512,1024]{1,0:T(8,128)S(1)} fusion(f32[16,1024]{1,0:T(8,128)S(1)} %get-tuple-element.218, f32[16,4096]{1,0:T(8,128)S(1)} %get-tuple-element.217, s32[]{:T(128)S(6)} %select_n.11), kind=kOutput, calls=%fused_computation.13.clone.1 | convolution fusion | flops 100663296 | bytes 2195460 | tf_op jit(solution)/shard_map/while/body/eval_jaxpr/dot_general | solution.py:55
  60.3 2.5 %fusion.41 = f32[33,4096]{1,0:T(8,128)S(1)} fusion(f32[33,4096]{1,0:T(8,128)S(1)} %get-tuple-element.203, s32[]{:T(128)S(6)} %select_n.11, f32[33,1024]{1,0:T(8,128)S(1)} %get-tuple-element.219, f32[512,1024]{1,0:T(8,128)S(1)} %fusion.40, f32[1024]{0:T(1024)S(1)} %get-tuple-element.216, f32[512]{0:T(512)S(1)} %dynamic_slice.29), kind=kOutput, calls=%fused_computation.8.clone.1 | convolution fusion | flops 209732096 | bytes 2430980 | tf_op jit(solution)/shard_map/while/body/eval_jaxpr/dot_general | solution.py:63
  62.8 1.8 %fusion.40 = f32[512,1024]{1,0:T(8,128)S(1)} fusion(f32[16,1024]{1,0:T(8,128)S(1)} %get-tuple-element.218, f32[16,4096]{1,0:T(8,128)S(1)} %get-tuple-element.217, s32[]{:T(128)S(6)} %select_n.11), kind=kOutput, calls=%fused_computation.13.clone.1 | convolution fusion | flops 100663296 | bytes 2195460 | tf_op jit(solution)/shard_map/while/body/eval_jaxpr/dot_general | solution.py:55
  64.7 2.5 %fusion.41 = f32[33,4096]{1,0:T(8,128)S(1)} fusion(f32[33,4096]{1,0:T(8,128)S(1)} %get-tuple-element.203, s32[]{:T(128)S(6)} %select_n.11, f32[33,1024]{1,0:T(8,128)S(1)} %get-tuple-element.219, f32[512,1024]{1,0:T(8,128)S(1)} %fusion.40, f32[1024]{0:T(1024)S(1)} %get-tuple-element.216, f32[512]{0:T(512)S(1)} %dynamic_slice.29), kind=kOutput, calls=%fused_computation.8.clone.1 | convolution fusion | flops 209732096 | bytes 2430980 | tf_op jit(solution)/shard_map/while/body/eval_jaxpr/dot_general | solution.py:63
  67.3 1.8 %fusion.40 = f32[512,1024]{1,0:T(8,128)S(1)} fusion(f32[16,1024]{1,0:T(8,128)S(1)} %get-tuple-element.218, f32[16,4096]{1,0:T(8,128)S(1)} %get-tuple-element.217, s32[]{:T(128)S(6)} %select_n.11), kind=kOutput, calls=%fused_computation.13.clone.1 | convolution fusion | flops 100663296 | bytes 2195460 | tf_op jit(solution)/shard_map/while/body/eval_jaxpr/dot_general | solution.py:55
  69.2 2.5 %fusion.41 = f32[33,4096]{1,0:T(8,128)S(1)} fusion(f32[33,4096]{1,0:T(8,128)S(1)} %get-tuple-element.203, s32[]{:T(128)S(6)} %select_n.11, f32[33,1024]{1,0:T(8,128)S(1)} %get-tuple-element.219, f32[512,1024]{1,0:T(8,128)S(1)} %fusion.40, f32[1024]{0:T(1024)S(1)} %get-tuple-element.216, f32[512]{0:T(512)S(1)} %dynamic_slice.29), kind=kOutput, calls=%fused_computation.8.clone.1 | convolution fusion | flops 209732096 | bytes 2430980 | tf_op jit(solution)/shard_map/while/body/eval_jaxpr/dot_general | solution.py:63
  71.7 1.8 %fusion.40 = f32[512,1024]{1,0:T(8,128)S(1)} fusion(f32[16,1024]{1,0:T(8,128)S(1)} %get-tuple-element.218, f32[16,4096]{1,0:T(8,128)S(1)} %get-tuple-element.217, s32[]{:T(128)S(6)} %select_n.11), kind=kOutput, calls=%fused_computation.13.clone.1 | convolution fusion | flops 100663296 | bytes 2195460 | tf_op jit(solution)/shard_map/while/body/eval_jaxpr/dot_general | solution.py:55
  73.7 2.5 %fusion.41 = f32[33,4096]{1,0:T(8,128)S(1)} fusion(f32[33,4096]{1,0:T(8,128)S(1)} %get-tuple-element.203, s32[]{:T(128)S(6)} %select_n.11, f32[33,1024]{1,0:T(8,128)S(1)} %get-tuple-element.219, f32[512,1024]{1,0:T(8,128)S(1)} %fusion.40, f32[1024]{0:T(1024)S(1)} %get-tuple-element.216, f32[512]{0:T(512)S(1)} %dynamic_slice.29), kind=kOutput, calls=%fused_computation.8.clone.1 | convolution fusion | flops 209732096 | bytes 2430980 | tf_op jit(solution)/shard_map/while/body/eval_jaxpr/dot_general | solution.py:63
  76.2 1.8 %fusion.40 = f32[512,1024]{1,0:T(8,128)S(1)} fusion(f32[16,1024]{1,0:T(8,128)S(1)} %get-tuple-element.218, f32[16,4096]{1,0:T(8,128)S(1)} %get-tuple-element.217, s32[]{:T(128)S(6)} %select_n.11), kind=kOutput, calls=%fused_computation.13.clone.1 | convolution fusion | flops 100663296 | bytes 2195460 | tf_op jit(solution)/shard_map/while/body/eval_jaxpr/dot_general | solution.py:55
  78.1 2.5 %fusion.41 = f32[33,4096]{1,0:T(8,128)S(1)} fusion(f32[33,4096]{1,0:T(8,128)S(1)} %get-tuple-element.203, s32[]{:T(128)S(6)} %select_n.11, f32[33,1024]{1,0:T(8,128)S(1)} %get-tuple-element.219, f32[512,1024]{1,0:T(8,128)S(1)} %fusion.40, f32[1024]{0:T(1024)S(1)} %get-tuple-element.216, f32[512]{0:T(512)S(1)} %dynamic_slice.29), kind=kOutput, calls=%fused_computation.8.clone.1 | convolution fusion | flops 209732096 | bytes 2430980 | tf_op jit(solution)/shard_map/while/body/eval_jaxpr/dot_general | solution.py:63
  80.7 1.8 %fusion.40 = f32[512,1024]{1,0:T(8,128)S(1)} fusion(f32[16,1024]{1,0:T(8,128)S(1)} %get-tuple-element.218, f32[16,4096]{1,0:T(8,128)S(1)} %get-tuple-element.217, s32[]{:T(128)S(6)} %select_n.11), kind=kOutput, calls=%fused_computation.13.clone.1 | convolution fusion | flops 100663296 | bytes 2195460 | tf_op jit(solution)/shard_map/while/body/eval_jaxpr/dot_general | solution.py:55
  82.6 2.5 %fusion.41 = f32[33,4096]{1,0:T(8,128)S(1)} fusion(f32[33,4096]{1,0:T(8,128)S(1)} %get-tuple-element.203, s32[]{:T(128)S(6)} %select_n.11, f32[33,1024]{1,0:T(8,128)S(1)} %get-tuple-element.219, f32[512,1024]{1,0:T(8,128)S(1)} %fusion.40, f32[1024]{0:T(1024)S(1)} %get-tuple-element.216, f32[512]{0:T(512)S(1)} %dynamic_slice.29), kind=kOutput, calls=%fused_computation.8.clone.1 | convolution fusion | flops 209732096 | bytes 2430980 | tf_op jit(solution)/shard_map/while/body/eval_jaxpr/dot_general | solution.py:63
  86.0 0.9 slice.37
  86.9 1.3 multiply_reduce_fusion
  88.3 39.4 %psum.7 = f32[16]{0:T(128)S(1)} all-reduce(f32[16]{0:T(128)S(1)} %multiply_reduce_fusion), channel_id=1, replica_groups=mesh['row'=4,'col'=8] {'row','col'}, use_global_device_ids=true, to_apply=%region_6.0 | all-reduce | flops 16 | bytes 128 | tf_op jit(solution)/shard_map/psum | solution.py:78
  128.2 22.2 %reduce-scatter.2.cloned.1.call-done = f32[33,512]{1,0:T(8,128)} async-done(((f32[33,4096]{1,0:T(8,128)}), f32[33,512]{1,0:T(8,128)}) %reduce-scatter.2.cloned.1.call-update) | async-done | bytes 67600 | tf_op jit(solution)/shard_map/reduce_scatter | solution.py:74
  151.2 1.6 fusion.24
  (32 shorter events, 6.6 us)
Async XLA Ops:
  7.2 143.3 %reduce-scatter.2.cloned.1.call-start = ((), (), s32[]{:S(2)}) async-start(), calls=%async_computation.1 | async-start | bytes 737280 | tf_op jit(solution)/shard_map/reduce_scatter | solution.py:74
  49.3 78.8 %copy-start.3 = (f32[512]{0:T(512)S(1)}, f32[512]{0:T(512)}, u32[]{:S(2)}) copy-start(f32[512]{0:T(512)} %param.8) | copy-start | bytes 6148
  49.4 101.8 %copy-start.1 = (f32[16,512]{1,0:T(8,128)S(1)}, f32[16,512]{1,0:T(8,128)}, u32[]{:S(2)}) copy-start(f32[16,512]{1,0:T(8,128)} %param.7) | copy-start | bytes 98308
  85.2 0.8 copy-start
  151.2 1.6 copy-start.2
Sparse Core Ops, SparseCore 0:
  86.1 64.2 reduce-scatter.1
where the time goes:
time: 160 us
  blocking collectives  77.7 us (49%)
  matrix products  34.8 us (22%)
  waiting for transfers between devices  22.3 us (14%)
  between operations  14.1 us (9%)
  other arithmetic  7.18 us (4%)
  local copies, waits for them, and re-layouts  3.16 us (2%)
    psum x1, blocking collectives, on_device(): grad = lax.psum(jnp.sum(tile_terms, 1), ('row', 'col')) / total_rows  39.4 us
    all_gather x1, blocking collectives, on_device(): gathered = lax.all_gather(own_rows, 'col', axis=1, tiled=True)  32 us
    reduce_scatter x1, waiting for transfers between devices, on_device(): summed = lax.psum_scatter(partials, 'col', scatter_dimension=1, tiled=True)  22.2 us
    dot_general x8, matrix products, add_block(): lax.dot_general(values, kernel, (((1,), (1,)), ((), ())), precision=lax.P...  20.1 us
    dot_general x8, matrix products, add_block(): lax.dot_general(row_block, col_scaled, (((0,), (0,)), ((), ())), precisio...  14.7 us
    all_gather x1, blocking collectives, on_device(): shard_piece = lax.all_gather(own_cols, 'row', axis=1, tiled=True)  6.32 us
  transfers between devices with their start and end apart: 1, of which 1 were waited for; matrix products, arithmetic and copies ran while one was open for 2% of the time, Pallas kernels for 0%

commit v1 on v0

--- a/solution.py
+++ b/solution.py
@@ -26,7 +26,19 @@
     inverse_scale = 1.0 / lengthscale
     own_scaled = x_rows * inverse_scale[:, None]
     own_rows = jnp.concatenate([own_scaled, alpha_rows[None, :]], 0)
-    gathered = lax.all_gather(own_rows, "col", axis=1, tiled=True)
+
+    def fit_the_ranges(local_values):
+        sides = jax.lax.axis_size("col")
+        e_now = local_values
+        r2 = [(k - 1, k) for k in range(1, sides)] + [(sides - 1, 0)]
+        in_order = [e_now]
+        for _ in range(sides - 1):
+            e_now = jax.lax.ppermute(e_now, "col", r2)
+            in_order += [e_now]
+        x_next = jnp.concatenate([*reversed(in_order)], axis=1)
+        return jnp.roll(x_next, (jax.lax.axis_index("col") + 1) * e_now.shape[1], axis=1)
+
+    gathered = fit_the_ranges(own_rows)
     row_scaled = gathered[:dims]
     row_alpha = gathered[dims]
     row_count = row_scaled.shape[1]

time: 160 us -> 167 us (1.044)
  waiting for transfers between devices: 22.3 us -> 60.2 us
  blocking collectives: 77.7 us -> 42.4 us
  starting transfers between devices: 0.04 us -> 3.05 us
    ppermute x0 -> x7, waiting for transfers between devices: none -> 39 us  [fit_the_ranges(): e_now = jax.lax.ppermute(e_now, 'col', r2)]
    all_gather x1 -> x0, blocking collectives: 32 us -> none  [on_device(): gathered = lax.all_gather(own_rows, 'col', axis=1, tiled=True)]
    ppermute x0 -> x7, starting transfers between devices: none -> 3.01 us  [fit_the_ranges(): e_now = jax.lax.ppermute(e_now, 'col', r2)]
    psum x1, blocking collectives: 39.4 us -> 37.1 us  [on_device(): grad = lax.psum(jnp.sum(tile_terms, 1), ('row', 'col')) / total_rows]
  transfers between devices with their start and end apart: 1 -> 8, of which waited for: 1 -> 8; matrix products, arithmetic and copies ran while one was open for 2% -> 3% of each run, Pallas kernels for 0% -> 0%
where the time goes in v1:
time: 167 us; the launch traced here: 166 us
  waiting for transfers between devices  60.2 us (36%)
  blocking collectives  42.4 us (25%)
  matrix products  34.9 us (21%)
  between operations  14.2 us (9%)
  other arithmetic  7.88 us (5%)
  local copies, waits for them, and re-layouts  3.24 us (2%)
  starting transfers between devices  3.05 us (2%)
    ppermute x7, waiting for transfers between devices, fit_the_ranges(): e_now = jax.lax.ppermute(e_now, 'col', r2)  39 us
    psum x1, blocking collectives, on_device(): grad = lax.psum(jnp.sum(tile_terms, 1), ('row', 'col')) / total_rows  37.1 us
    reduce_scatter x1, waiting for transfers between devices, on_device(): summed = lax.psum_scatter(partials, 'col', scatter_dimension=1, tiled=True)  21.2 us
    dot_general x8, matrix products, add_block(): lax.dot_general(values, kernel, (((1,), (1,)), ((), ())), precision=lax.P...  20.2 us
    dot_general x8, matrix products, add_block(): lax.dot_general(row_block, col_scaled, (((0,), (0,)), ((), ())), precisio...  14.7 us
    all_gather x1, blocking collectives, on_device(): shard_piece = lax.all_gather(own_cols, 'row', axis=1, tiled=True)  5.31 us
  transfers between devices with their start and end apart: 8, of which 8 were waited for; matrix products, arithmetic and copies ran while one was open for 3% of the time, Pallas kernels for 0%

profile of v1, /device:TPU:0, one launch (start us, length us, event | category | flops | bytes accessed | tf_op | source)
XLA Modules:
  0.0 166.2 jit_solution(17845357251310154505)
XLA Ops:
  9.4 3.0 %collective-permute-start = (f32[17,512]{1,0:T(8,128)S(1)}, f32[17,512]{1,0:T(8,128)S(1)}, u32[]{:S(2)}, u32[]{:S(2)}) collective-permute-start(f32[17,512]{1,0:T(8,128)S(1)} %pad_maximum_fusion.1), channel_id=1, source_target_pairs={{0,1},{1,2},{2,3},{3,4},{4,5},{5,6},{6,7},{7,0},{8,9},{9,10},{10,1... | collective-permute-start | bytes 104456 | tf_op jit(solution)/shard_map/ppermute | solution.py:36
  12.4 5.1 %collective-permute-done = f32[17,512]{1,0:T(8,128)S(1)} collective-permute-done((f32[17,512]{1,0:T(8,128)S(1)}, f32[17,512]{1,0:T(8,128)S(1)}, u32[]{:S(2)}, u32[]{:S(2)}) %collective-permute-start) | collective-permute-done | bytes 34848 | tf_op jit(solution)/shard_map/ppermute | solution.py:36
  17.5 6.8 %collective-permute-done.1 = f32[17,512]{1,0:T(8,128)S(1)} collective-permute-done((f32[17,512]{1,0:T(8,128)S(1)}, f32[17,512]{1,0:T(8,128)S(1)}, u32[]{:S(2)}, u32[]{:S(2)}) %collective-permute-start.1) | collective-permute-done | bytes 34848 | tf_op jit(solution)/shard_map/ppermute | solution.py:36
  24.3 6.8 %collective-permute-done.2 = f32[17,512]{1,0:T(8,128)S(1)} collective-permute-done((f32[17,512]{1,0:T(8,128)S(1)}, f32[17,512]{1,0:T(8,128)S(1)}, u32[]{:S(2)}, u32[]{:S(2)}) %collective-permute-start.2) | collective-permute-done | bytes 34848 | tf_op jit(solution)/shard_map/ppermute | solution.py:36
  31.9 6.0 %collective-permute-done.3 = f32[17,512]{1,0:T(8,128)S(1)} collective-permute-done((f32[17,512]{1,0:T(8,128)S(1)}, f32[17,512]{1,0:T(8,128)S(1)}, u32[]{:S(2)}, u32[]{:S(2)}) %collective-permute-start.3) | collective-permute-done | bytes 34848 | tf_op jit(solution)/shard_map/ppermute | solution.py:36
  38.6 5.3 %all_gather.3 = f32[17,1024]{1,0:T(8,128)S(1)} all-gather(f32[17,256]{1,0:T(8,128)S(1)} %pad_maximum_fusion.2), channel_id=1, replica_groups=mesh['row'=4,'col'=8] {'row'}, dimensions={1}, use_global_device_ids=true | all-gather | bytes 87040 | tf_op jit(solution)/shard_map/all_gather | solution.py:50
  44.7 6.8 %collective-permute-done.5 = f32[17,512]{1,0:T(8,128)S(1)} collective-permute-done((f32[17,512]{1,0:T(8,128)S(1)}, f32[17,512]{1,0:T(8,128)S(1)}, u32[]{:S(2)}, u32[]{:S(2)}) %collective-permute-start.5) | collective-permute-done | bytes 34848 | tf_op jit(solution)/shard_map/ppermute | solution.py:36
  51.5 6.7 %collective-permute-done.6 = f32[17,512]{1,0:T(8,128)S(1)} collective-permute-done((f32[17,512]{1,0:T(8,128)S(1)}, f32[17,512]{1,0:T(8,128)S(1)}, u32[]{:S(2)}, u32[]{:S(2)}) %collective-permute-start.6) | collective-permute-done | bytes 34848 | tf_op jit(solution)/shard_map/ppermute | solution.py:36
  59.2 35.8 %while.13 = (s32[]{:T(128)}, f32[33,4096]{1,0:T(8,128)S(1)}, f32[4096]{0:T(1024)S(1)}, f32[1024]{0:T(1024)S(1)}, f32[16,4096]{1,0:T(8,128)S(1)}, /*index=5*/f32[...) while((s32[]{:T(128)}, f32[33,4096]{1,0:T(8,128)S(1)}, ...), condition=%wide.region_3.4_spmd, body=%wide.region_2.3_spmd.sunk | while | flops 310395392 | bytes 4630695 | solution.py:85
  59.3 1.8 %fusion.39 = f32[512,1024]{1,0:T(8,128)S(1)} fusion(f32[16,1024]{1,0:T(8,128)S(1)} %get-tuple-element.218, f32[16,4096]{1,0:T(8,128)S(1)} %get-tuple-element.217, s32[]{:T(128)S(6)} %select_n.26), kind=kOutput, calls=%fused_computation.13.clone.1 | convolution fusion | flops 100663296 | bytes 2195460 | tf_op jit(solution)/shard_map/while/body/eval_jaxpr/dot_general | solution.py:67
  61.2 2.5 %fusion.40 = f32[33,4096]{1,0:T(8,128)S(1)} fusion(f32[33,4096]{1,0:T(8,128)S(1)} %get-tuple-element.203, s32[]{:T(128)S(6)} %select_n.26, f32[33,1024]{1,0:T(8,128)S(1)} %get-tuple-element.219, f32[512,1024]{1,0:T(8,128)S(1)} %fusion.39, f32[1024]{0:T(1024)S(1)} %get-tuple-element.216, f32[512]{0:T(512)S(1)} %dynamic_slice.34), kind=kOutput, calls=%fused_computation.8.clone.1 | convolution fusion | flops 209732096 | bytes 2430980 | tf_op jit(solution)/shard_map/while/body/eval_jaxpr/dot_general | solution.py:75
  65.7 2.5 %fusion.40 = f32[33,4096]{1,0:T(8,128)S(1)} fusion(f32[33,4096]{1,0:T(8,128)S(1)} %get-tuple-element.203, s32[]{:T(128)S(6)} %select_n.26, f32[33,1024]{1,0:T(8,128)S(1)} %get-tuple-element.219, f32[512,1024]{1,0:T(8,128)S(1)} %fusion.39, f32[1024]{0:T(1024)S(1)} %get-tuple-element.216, f32[512]{0:T(512)S(1)} %dynamic_slice.34), kind=kOutput, calls=%fused_computation.8.clone.1 | convolution fusion | flops 209732096 | bytes 2430980 | tf_op jit(solution)/shard_map/while/body/eval_jaxpr/dot_general | solution.py:75
  68.3 1.8 %fusion.39 = f32[512,1024]{1,0:T(8,128)S(1)} fusion(f32[16,1024]{1,0:T(8,128)S(1)} %get-tuple-element.218, f32[16,4096]{1,0:T(8,128)S(1)} %get-tuple-element.217, s32[]{:T(128)S(6)} %select_n.26), kind=kOutput, calls=%fused_computation.13.clone.1 | convolution fusion | flops 100663296 | bytes 2195460 | tf_op jit(solution)/shard_map/while/body/eval_jaxpr/dot_general | solution.py:67
  70.1 2.5 %fusion.40 = f32[33,4096]{1,0:T(8,128)S(1)} fusion(f32[33,4096]{1,0:T(8,128)S(1)} %get-tuple-element.203, s32[]{:T(128)S(6)} %select_n.26, f32[33,1024]{1,0:T(8,128)S(1)} %get-tuple-element.219, f32[512,1024]{1,0:T(8,128)S(1)} %fusion.39, f32[1024]{0:T(1024)S(1)} %get-tuple-element.216, f32[512]{0:T(512)S(1)} %dynamic_slice.34), kind=kOutput, calls=%fused_computation.8.clone.1 | convolution fusion | flops 209732096 | bytes 2430980 | tf_op jit(solution)/shard_map/while/body/eval_jaxpr/dot_general | solution.py:75
  74.6 2.5 %fusion.40 = f32[33,4096]{1,0:T(8,128)S(1)} fusion(f32[33,4096]{1,0:T(8,128)S(1)} %get-tuple-element.203, s32[]{:T(128)S(6)} %select_n.26, f32[33,1024]{1,0:T(8,128)S(1)} %get-tuple-element.219, f32[512,1024]{1,0:T(8,128)S(1)} %fusion.39, f32[1024]{0:T(1024)S(1)} %get-tuple-element.216, f32[512]{0:T(512)S(1)} %dynamic_slice.34), kind=kOutput, calls=%fused_computation.8.clone.1 | convolution fusion | flops 209732096 | bytes 2430980 | tf_op jit(solution)/shard_map/while/body/eval_jaxpr/dot_general | solution.py:75
  77.2 1.8 %fusion.39 = f32[512,1024]{1,0:T(8,128)S(1)} fusion(f32[16,1024]{1,0:T(8,128)S(1)} %get-tuple-element.218, f32[16,4096]{1,0:T(8,128)S(1)} %get-tuple-element.217, s32[]{:T(128)S(6)} %select_n.26), kind=kOutput, calls=%fused_computation.13.clone.1 | convolution fusion | flops 100663296 | bytes 2195460 | tf_op jit(solution)/shard_map/while/body/eval_jaxpr/dot_general | solution.py:67
  79.1 2.5 %fusion.40 = f32[33,4096]{1,0:T(8,128)S(1)} fusion(f32[33,4096]{1,0:T(8,128)S(1)} %get-tuple-element.203, s32[]{:T(128)S(6)} %select_n.26, f32[33,1024]{1,0:T(8,128)S(1)} %get-tuple-element.219, f32[512,1024]{1,0:T(8,128)S(1)} %fusion.39, f32[1024]{0:T(1024)S(1)} %get-tuple-element.216, f32[512]{0:T(512)S(1)} %dynamic_slice.34), kind=kOutput, calls=%fused_computation.8.clone.1 | convolution fusion | flops 209732096 | bytes 2430980 | tf_op jit(solution)/shard_map/while/body/eval_jaxpr/dot_general | solution.py:75
  83.5 2.5 %fusion.40 = f32[33,4096]{1,0:T(8,128)S(1)} fusion(f32[33,4096]{1,0:T(8,128)S(1)} %get-tuple-element.203, s32[]{:T(128)S(6)} %select_n.26, f32[33,1024]{1,0:T(8,128)S(1)} %get-tuple-element.219, f32[512,1024]{1,0:T(8,128)S(1)} %fusion.39, f32[1024]{0:T(1024)S(1)} %get-tuple-element.216, f32[512]{0:T(512)S(1)} %dynamic_slice.34), kind=kOutput, calls=%fused_computation.8.clone.1 | convolution fusion | flops 209732096 | bytes 2430980 | tf_op jit(solution)/shard_map/while/body/eval_jaxpr/dot_general | solution.py:75
  86.2 1.8 %fusion.39 = f32[512,1024]{1,0:T(8,128)S(1)} fusion(f32[16,1024]{1,0:T(8,128)S(1)} %get-tuple-element.218, f32[16,4096]{1,0:T(8,128)S(1)} %get-tuple-element.217, s32[]{:T(128)S(6)} %select_n.26), kind=kOutput, calls=%fused_computation.13.clone.1 | convolution fusion | flops 100663296 | bytes 2195460 | tf_op jit(solution)/shard_map/while/body/eval_jaxpr/dot_general | solution.py:67
  88.0 2.5 %fusion.40 = f32[33,4096]{1,0:T(8,128)S(1)} fusion(f32[33,4096]{1,0:T(8,128)S(1)} %get-tuple-element.203, s32[]{:T(128)S(6)} %select_n.26, f32[33,1024]{1,0:T(8,128)S(1)} %get-tuple-element.219, f32[512,1024]{1,0:T(8,128)S(1)} %fusion.39, f32[1024]{0:T(1024)S(1)} %get-tuple-element.216, f32[512]{0:T(512)S(1)} %dynamic_slice.34), kind=kOutput, calls=%fused_computation.8.clone.1 | convolution fusion | flops 209732096 | bytes 2430980 | tf_op jit(solution)/shard_map/while/body/eval_jaxpr/dot_general | solution.py:75
  90.6 1.8 %fusion.39 = f32[512,1024]{1,0:T(8,128)S(1)} fusion(f32[16,1024]{1,0:T(8,128)S(1)} %get-tuple-element.218, f32[16,4096]{1,0:T(8,128)S(1)} %get-tuple-element.217, s32[]{:T(128)S(6)} %select_n.26), kind=kOutput, calls=%fused_computation.13.clone.1 | convolution fusion | flops 100663296 | bytes 2195460 | tf_op jit(solution)/shard_map/while/body/eval_jaxpr/dot_general | solution.py:67
  92.5 2.5 %fusion.40 = f32[33,4096]{1,0:T(8,128)S(1)} fusion(f32[33,4096]{1,0:T(8,128)S(1)} %get-tuple-element.203, s32[]{:T(128)S(6)} %select_n.26, f32[33,1024]{1,0:T(8,128)S(1)} %get-tuple-element.219, f32[512,1024]{1,0:T(8,128)S(1)} %fusion.39, f32[1024]{0:T(1024)S(1)} %get-tuple-element.216, f32[512]{0:T(512)S(1)} %dynamic_slice.34), kind=kOutput, calls=%fused_computation.8.clone.1 | convolution fusion | flops 209732096 | bytes 2430980 | tf_op jit(solution)/shard_map/while/body/eval_jaxpr/dot_general | solution.py:75
  98.2 37.1 %psum.7 = f32[16]{0:T(128)S(1)} all-reduce(f32[16]{0:T(128)S(1)} %multiply_reduce_fusion), channel_id=1, replica_groups=mesh['row'=4,'col'=8] {'row','col'}, use_global_device_ids=true, to_apply=%region_6.7 | all-reduce | flops 16 | bytes 128 | tf_op jit(solution)/shard_map/psum | solution.py:90
  135.8 21.2 %reduce-scatter.2.cloned.1.call-done = f32[33,512]{1,0:T(8,128)} async-done(((f32[33,4096]{1,0:T(8,128)}), f32[33,512]{1,0:T(8,128)}) %reduce-scatter.2.cloned.1.call-update) | async-done | bytes 67600 | tf_op jit(solution)/shard_map/reduce_scatter | solution.py:86
  (61 shorter events, 17.5 us)
Async XLA Ops:
  7.2 51.9 %copy-start.2 = (f32[512]{0:T(512)S(1)}, f32[512]{0:T(512)}, u32[]{:S(2)}) copy-start(f32[512]{0:T(512)} %param.8) | copy-start | bytes 6148
  7.2 149.9 %reduce-scatter.2.cloned.1.call-start = ((), (), s32[]{:S(2)}) async-start(), calls=%async_computation.1 | async-start | bytes 737280 | tf_op jit(solution)/shard_map/reduce_scatter | solution.py:86
  9.4 8.1 %collective-permute-start = (f32[17,512]{1,0:T(8,128)S(1)}, f32[17,512]{1,0:T(8,128)S(1)}, u32[]{:S(2)}, u32[]{:S(2)}) collective-permute-start(f32[17,512]{1,0:T(8,128)S(1)} %pad_maximum_fusion.1), channel_id=1, source_target_pairs={{0,1},{1,2},{2,3},{3,4},{4,5},{5,6},{6,7},{7,0},{8,9},{9,10},{10,1... | collective-permute-start | bytes 104456 | tf_op jit(solution)/shard_map/ppermute | solution.py:36
  17.5 6.8 %collective-permute-start.1 = (f32[17,512]{1,0:T(8,128)S(1)}, f32[17,512]{1,0:T(8,128)S(1)}, u32[]{:S(2)}, u32[]{:S(2)}) collective-permute-start(f32[17,512]{1,0:T(8,128)S(1)} %collective-permute-done), channel_id=1, source_target_pairs={{0,1},{1,2},{2,3},{3,4},{4,5},{5,6},{6,7},{7,0},{8,9},{9,10},{10,1... | collective-permute-start | bytes 104456 | tf_op jit(solution)/shard_map/ppermute | solution.py:36
  24.3 6.8 %collective-permute-start.2 = (f32[17,512]{1,0:T(8,128)S(1)}, f32[17,512]{1,0:T(8,128)S(1)}, u32[]{:S(2)}, u32[]{:S(2)}) collective-permute-start(f32[17,512]{1,0:T(8,128)S(1)} %collective-permute-done.1), channel_id=1, source_target_pairs={{0,1},{1,2},{2,3},{3,4},{4,5},{5,6},{6,7},{7,0},{8,9},{9,10},{10,1... | collective-permute-start | bytes 104456 | tf_op jit(solution)/shard_map/ppermute | solution.py:36
  31.1 6.8 %collective-permute-start.3 = (f32[17,512]{1,0:T(8,128)S(1)}, f32[17,512]{1,0:T(8,128)S(1)}, u32[]{:S(2)}, u32[]{:S(2)}) collective-permute-start(f32[17,512]{1,0:T(8,128)S(1)} %collective-permute-done.2), channel_id=1, source_target_pairs={{0,1},{1,2},{2,3},{3,4},{4,5},{5,6},{6,7},{7,0},{8,9},{9,10},{10,1... | collective-permute-start | bytes 104456 | tf_op jit(solution)/shard_map/ppermute | solution.py:36
  37.9 6.8 %collective-permute-start.4 = (f32[17,512]{1,0:T(8,128)S(1)}, f32[17,512]{1,0:T(8,128)S(1)}, u32[]{:S(2)}, u32[]{:S(2)}) collective-permute-start(f32[17,512]{1,0:T(8,128)S(1)} %collective-permute-done.3), channel_id=1, source_target_pairs={{0,1},{1,2},{2,3},{3,4},{4,5},{5,6},{6,7},{7,0},{8,9},{9,10},{10,1... | collective-permute-start | bytes 104456 | tf_op jit(solution)/shard_map/ppermute | solution.py:36
  44.7 6.8 %collective-permute-start.5 = (f32[17,512]{1,0:T(8,128)S(1)}, f32[17,512]{1,0:T(8,128)S(1)}, u32[]{:S(2)}, u32[]{:S(2)}) collective-permute-start(f32[17,512]{1,0:T(8,128)S(1)} %collective-permute-done.4), channel_id=1, source_target_pairs={{0,1},{1,2},{2,3},{3,4},{4,5},{5,6},{6,7},{7,0},{8,9},{9,10},{10,1... | collective-permute-start | bytes 104456 | tf_op jit(solution)/shard_map/ppermute | solution.py:36
  51.4 6.8 %collective-permute-start.6 = (f32[17,512]{1,0:T(8,128)S(1)}, f32[17,512]{1,0:T(8,128)S(1)}, u32[]{:S(2)}, u32[]{:S(2)}) collective-permute-start(f32[17,512]{1,0:T(8,128)S(1)} %collective-permute-done.5), channel_id=1, source_target_pairs={{0,1},{1,2},{2,3},{3,4},{4,5},{5,6},{6,7},{7,0},{8,9},{9,10},{10,1... | collective-permute-start | bytes 104456 | tf_op jit(solution)/shard_map/ppermute | solution.py:36
  59.2 98.5 %copy-start.1 = (f32[16,512]{1,0:T(8,128)S(1)}, f32[16,512]{1,0:T(8,128)}, u32[]{:S(2)}) copy-start(f32[16,512]{1,0:T(8,128)} %param.7) | copy-start | bytes 98308
  95.0 0.8 copy-start
  157.8 1.6 copy-start.3
Sparse Core Ops, SparseCore 0:
  96.0 60.9 reduce-scatter.1
